TPU v7x, 512 devices: a whole 4x8x8 slice. The times are simulated.
512 devices in a mesh: wide: 64 (over z_hi, y, core), narrow: 8 (over x, z_lo).
Axes of the slice: x: 4, y: 8, z: 8 (z_hi: 4, z_lo: 2; z = z_hi * 2 + z_lo), core: 2. Of those that a mesh axis runs over, the one named last changes fastest.
Arguments:
- enc_hidden: bfloat16 [12288, 6144], P('wide', 'narrow'), may hold values from -6 to 6
- enc_gain: float32 [6144], P('narrow'), may hold values from 0.1 to 1.9
- cross_weight: bfloat16 [6144, 256], P('narrow'), may hold values from -0.078125 to 0.078125
- assign: int32 [64], P('wide'), may hold values from 0 to 7
- token_ids: int32 [64, 2, 64], P('wide'), may hold values from 0 to 7999, as said below
- cross_table: bfloat16 [8000, 6144], P('wide', 'narrow'), may hold values from -540 to 540
- self_table: bfloat16 [8000, 6144], P('wide', 'narrow'), may hold values from -540 to 540
- kv_table: bfloat16 [8000, 256], P('wide'), may hold values from -6 to 6
- self_cache: bfloat16 [64, 64, 768, 256], P('wide', 'narrow'), may hold values from -6 to 6
Outputs:
- cross_out: bfloat16 [64, 2, 64, 6144], P('wide', None, None, 'narrow')
- self_out: bfloat16 [64, 2, 64, 6144], P('wide', None, 'narrow')
Inputs may be any that keep to these rules, and one draw needn't show every extreme that they name: `token_ids`: within one group, at most 4 of its 128 ids lie in any one of the 64 ranges of 125 consecutive ids, and some range holds exactly 4 of them.
All inputs are finite; a program needn't handle non-finite values.
Results may differ from a plain program's by a relative error of at most 0.009.
The roundings to bfloat16 on the way count: a program that leaves them out, or rounds other values in their place, can miss the bound.
Values may be sent and summed in bfloat16 or wider, within the bound.
No kernel may reach another device: no remote copies, remote signals or barrier semaphores. Data moves between devices by JAX's collectives and lax.ppermute only.
A program may use at most 64 MiB of HBM per device.

v0:
```python
import jax
import jax.numpy as jnp
from jax import lax
from jax.sharding import PartitionSpec as P

D = 6144
HEADS = 48
HEAD = 128
OWN = 8
ENC_LEN = 1536
EPS = 1e-06


def cut_along(shard, dim, length):
    shape = shard.shape
    pieces = shard.reshape(*shape[:dim], length, shape[dim] // length, *shape[dim + 1 :])
    return jnp.moveaxis(pieces, dim, 0)


def sent_and_summed(shard, axis, dim):
    pieces = cut_along(shard, dim, lax.axis_size(axis))
    arrived = lax.all_to_all(pieces, axis, split_axis=0, concat_axis=0, tiled=True)
    return arrived.sum(axis=0)


def sent_together(arrays, axis, dim, along):
    columns = [a.reshape(*a.shape[:along], -1) for a in arrays]
    both = jnp.concatenate(columns, axis=along)
    whole, at, outs = (sent_and_summed(both, axis, dim), 0, [])
    for a, column in zip(arrays, columns):
        piece = whole[..., at : at + column.shape[along]]
        outs.append(piece.reshape(*piece.shape[:along], *a.shape[along:]))
        at += column.shape[along]
    return tuple(outs)


def copy_for_each(shard, axis):
    length = lax.axis_size(axis)
    return lax.all_to_all(
        jnp.broadcast_to(shard[None], (length, *shard.shape)), axis, 0, 0, tiled=True
    )


def joined_along(pieces, dim):
    shape = list(pieces.shape[1:])
    shape[dim] *= pieces.shape[0]
    return jnp.moveaxis(pieces, 0, dim).reshape(shape)


def gather_directly(shard, axis, dim):
    pieces = copy_for_each(shard, axis)
    return joined_along(pieces, dim)


def in_one_piece(arrays, axis, split_dim, concat_dim, along):
    both = jnp.concatenate(arrays, axis=along)
    whole, at, outs = (
        lax.all_to_all(both, axis, split_axis=split_dim, concat_axis=concat_dim, tiled=True),
        0,
        [],
    )
    for a in arrays:
        outs.append(lax.slice_in_dim(whole, at, at + a.shape[along], axis=along))
        at += a.shape[along]
    return tuple(outs)


def body(
    enc_hidden,
    enc_gain,
    cross_weight,
    assign,
    token_ids,
    cross_table,
    self_table,
    kv_table,
    self_cache,
):
    hidden = enc_hidden.astype(jnp.float32)
    part_squares = jnp.sum(hidden * hidden, axis=1)
    scaled = (hidden * enc_gain).astype(jnp.bfloat16)
    part_proj = jnp.dot(scaled, cross_weight, preferred_element_type=jnp.float32)
    problem = assign[0]
    narrow_count = lax.axis_size("narrow")
    narrow_index = lax.axis_index("narrow")
    heads_dev = HEADS // narrow_count
    factor = HEAD ** (-0.5)
    projected, squares = sent_together((part_proj, part_squares), "narrow", 0, 1)
    enc_kv = (projected * lax.rsqrt(squares / D + EPS)[:, None]).astype(jnp.bfloat16)
    gathered = gather_directly(enc_kv, "wide", 0)
    span = ENC_LEN // narrow_count
    mine = lax.dynamic_slice_in_dim(gathered, problem * span, span, 0)
    mine = mine.reshape(OWN, span // OWN, 2 * HEAD)
    problem_kv = gather_directly(mine, "narrow", 1).reshape(ENC_LEN, 2 * HEAD)
    keys = problem_kv[:, :HEAD]
    values = problem_kv[:, HEAD:]
    wide_count = lax.axis_size("wide")
    per_owner = cross_table.shape[0]
    steps = token_ids.shape[1]
    cand = token_ids.shape[2]
    capacity = max(2, 2 * steps * cand // wide_count)
    flat = token_ids.reshape(-1)
    owner = flat // per_owner
    local = flat - owner * per_owner
    owner_hits = (owner[:, None] == jnp.arange(wide_count, dtype=jnp.int32)[None, :]).astype(
        jnp.int32
    )
    earlier = jnp.cumsum(owner_hits, axis=0) - owner_hits
    rank = jnp.sum(earlier * owner_hits, axis=1)
    target = owner * capacity + rank
    slot_match = target[None, :] == jnp.arange(wide_count * capacity, dtype=jnp.int32)[:, None]
    filled = jnp.any(slot_match, axis=1)
    request = jnp.where(filled, jnp.sum(jnp.where(slot_match, local[None, :], 0), axis=1), -1)
    asked = lax.all_to_all(
        request.reshape(wide_count, capacity), "wide", split_axis=0, concat_axis=0, tiled=True
    ).reshape(-1)
    valid = asked >= 0
    index = jnp.where(valid, asked, 0)

    def lookup(table):
        rows = jnp.take(table, index, axis=0)
        rows = jnp.where(valid[:, None], rows, jnp.zeros((), table.dtype))
        return rows.reshape(wide_count, capacity, table.shape[1])

    returned = in_one_piece(
        (lookup(cross_table), lookup(self_table), lookup(kv_table)), "wide", 0, 0, 2
    )
    cross_q, self_q, new_kv = [
        jnp.take(piece.reshape(wide_count * capacity, piece.shape[2]), target, axis=0)
        for piece in returned
    ]
    rows_total = steps * cand
    own_q = cross_q.reshape(rows_total, heads_dev, HEAD)
    scores = jnp.einsum("rhd,kd->rhk", own_q, keys, preferred_element_type=jnp.float32) * factor
    peak = jnp.max(scores, axis=-1, keepdims=True)
    expo = jnp.exp(scores - peak)
    total = jnp.sum(expo, axis=-1)
    result = (
        jnp.einsum(
            "rhk,kd->rhd", expo.astype(jnp.bfloat16), values, preferred_element_type=jnp.float32
        )
        / total[..., None]
    )
    cross_out = result.astype(jnp.bfloat16).reshape(1, steps, cand, heads_dev * HEAD)
    own_cand = cand // narrow_count
    queries = lax.all_to_all(
        self_q.reshape(steps, cand, self_q.shape[1]),
        "narrow",
        split_axis=1,
        concat_axis=2,
        tiled=True,
    )
    queries = queries.reshape(steps, own_cand, HEADS, HEAD)
    fresh = lax.dynamic_slice_in_dim(
        new_kv.reshape(steps, cand, new_kv.shape[1]), narrow_index * own_cand, own_cand, 1
    )
    cache = self_cache[0]
    prefix_scores = (
        jnp.einsum("tchd,cpd->tchp", queries, cache[..., :HEAD], preferred_element_type=jnp.float32)
        * factor
    )
    fresh_scores = (
        jnp.einsum("tchd,jcd->tchj", queries, fresh[..., :HEAD], preferred_element_type=jnp.float32)
        * factor
    )
    step_index = jnp.arange(steps, dtype=jnp.int32)
    allowed = (step_index[None, :] <= step_index[:, None])[:, None, None, :]
    fresh_masked = jnp.where(allowed, fresh_scores, -jnp.inf)
    peak = jnp.maximum(jnp.max(prefix_scores, axis=-1), jnp.max(fresh_masked, axis=-1))[..., None]
    prefix_expo = jnp.exp(prefix_scores - peak)
    fresh_expo = jnp.where(allowed, jnp.exp(fresh_masked - peak), 0.0)
    total = jnp.sum(prefix_expo, axis=-1) + jnp.sum(fresh_expo, axis=-1)
    summed = jnp.einsum(
        "tchp,cpd->tchd",
        prefix_expo.astype(jnp.bfloat16),
        cache[..., HEAD:],
        preferred_element_type=jnp.float32,
    )
    summed = summed + jnp.einsum(
        "tchj,jcd->tchd",
        fresh_expo.astype(jnp.bfloat16),
        fresh[..., HEAD:],
        preferred_element_type=jnp.float32,
    )
    self_result = summed / total[..., None]
    self_out = self_result.astype(jnp.bfloat16).reshape(1, steps, own_cand, HEADS * HEAD)
    return (cross_out, self_out)


def solution(mesh):
    placed = (
        P("wide", "narrow"),
        P("narrow"),
        P("narrow", None),
        P("wide"),
        P("wide", None, None),
        P("wide", "narrow"),
        P("wide", "narrow"),
        P("wide", None),
        P("wide", "narrow", None, None),
    )
    return jax.shard_map(
        body,
        mesh=mesh,
        in_specs=placed,
        out_specs=(P("wide", None, None, "narrow"), P("wide", None, "narrow", None)),
        check_vma=False,
    )
```

profile of v0, /device:TPU:24, one launch (start us, length us, event | category | flops | bytes accessed | tf_op | source)
XLA Modules:
  0.0 142.2 jit_solution(7858502208447242143)
XLA Ops:
  2.9 16.3 %all-to-all-start = ((s32[64,1,4]{2,1,0:T(1,128)}), s32[64,1,4]{2,1,0:T(1,128)S(1)}, u32[]{:S(2)}, u32[]{:S(2)}) async-start(s32[64,1,4]{2,1,0:T(1,128)} %bitcast), calls=%async_computation | async-start | bytes 65536 | tf_op jit(solution)/shard_map/all_to_all | solution.py:114
  19.3 1.1 fusion.27
  20.6 1.2 fusion.29
  22.6 6.0 %all-to-all-done = s32[64,1,4]{2,1,0:T(1,128)S(1)} async-done(((s32[64,1,4]{2,1,0:T(1,128)}), s32[64,1,4]{2,1,0:T(1,128)S(1)}, u32[]{:S(2)}, u32[]{:S(2)}) %all-to-all-start) | async-done | bytes 1056 | tf_op jit(solution)/shard_map/all_to_all | solution.py:114
  28.5 5.2 %all-to-all-start.2 = ((f32[8,24,257]{2,1,0:T(8,128)}), f32[8,24,257]{2,1,0:T(8,128)S(1)}, u32[]{:S(2)}, u32[]{:S(2)}) async-start(f32[8,24,257]{2,1,0:T(8,128)} %pad_maximum_fusion.1), calls=%async_computation.2 | async-start | bytes 589824 | tf_op jit(solution)/shard_map/all_to_all | solution.py:22
  35.3 1.2 gather_fusion
  36.5 1.2 gather_fusion.3
  37.7 1.2 gather_fusion.2
  39.5 1.3 pad_maximum_fusion
  41.4 7.2 %all-to-all-start.1 = ((bf16[64,4,1792]{2,1,0:T(4,128)(2,1)}), bf16[64,4,1792]{2,1,0:T(4,128)(2,1)S(1)}, u32[]{:S(2)}, u32[]{:S(2)}) async-start(bf16[64,4,1792]{2,1,0:T(4,128)(2,1)} %pad_maximum_fusion), calls=%async_computation.1 | async-start | bytes 1835008 | tf_op jit(solution)/shard_map/all_to_all | solution.py:58
  49.5 24.8 %all-to-all-done.1 = bf16[64,4,1792]{2,1,0:T(4,128)(2,1)S(1)} async-done(((bf16[64,4,1792]{2,1,0:T(4,128)(2,1)}), bf16[64,4,1792]{2,1,0:T(4,128)(2,1)S(1)}, u32[]{:S(2)}, u32[]{:S(2)}) %all-to-all-start.1) | async-done | bytes 917536 | tf_op jit(solution)/shard_map/all_to_all | solution.py:58
  74.4 0.9 broadcast_in_dim.142
  75.3 9.5 %all-to-all-start.3 = ((bf16[64,24,256]{2,1,0:T(8,128)(2,1)}), bf16[64,24,256]{2,1,0:T(8,128)(2,1)S(1)}, u32[]{:S(2)}, u32[]{:S(2)}) async-start(bf16[64,24,256]{2,1,0:T(8,128)(2,1)} %broadcast_in_dim.142), calls=%async_computation.3 | async-start | bytes 1572864 | tf_op jit(solution)/shard_map/all_to_all | solution.py:39
  89.4 18.6 %all-to-all-done.3 = bf16[64,24,256]{2,1,0:T(8,128)(2,1)S(1)} async-done(((bf16[64,24,256]{2,1,0:T(8,128)(2,1)}), bf16[64,24,256]{2,1,0:T(8,128)(2,1)S(1)}, u32[]{:S(2)}, u32[]{:S(2)}) %all-to-all-start.3) | async-done | bytes 786464 | tf_op jit(solution)/shard_map/all_to_all | solution.py:39
  108.0 4.8 %all-to-all-start.5 = ((bf16[2,64,768]{2,0,1:T(2,128)(2,1)}), bf16[2,64,768]{2,0,1:T(2,128)(2,1)S(1)}, u32[]{:S(2)}, u32[]{:S(2)}) async-start(bf16[2,64,768]{2,0,1:T(2,128)(2,1)} %copy.54), calls=%async_computation.5 | async-start | bytes 393216 | tf_op jit(solution)/shard_map/all_to_all | solution.py:146
  113.0 7.4 %all-to-all-done.5 = bf16[2,64,768]{2,0,1:T(2,128)(2,1)S(1)} async-done(((bf16[2,64,768]{2,0,1:T(2,128)(2,1)}), bf16[2,64,768]{2,0,1:T(2,128)(2,1)S(1)}, u32[]{:S(2)}, u32[]{:S(2)}) %all-to-all-start.5) | async-done | bytes 196640 | tf_op jit(solution)/shard_map/all_to_all | solution.py:146
  120.4 0.9 broadcast_in_dim.144
  121.3 3.7 %all-to-all-start.4 = ((bf16[8,8,24,256]{3,2,1,0:T(8,128)(2,1)}), bf16[8,8,24,256]{3,2,1,0:T(8,128)(2,1)S(1)}, u32[]{:S(2)}, u32[]{:S(2)}) async-start(bf16[8,8,24,256]{3,2,1,0:T(8,128)(2,1)} %broadcast_in_dim.144), calls=%async_computation.4 | async-start | bytes 1572864 | tf_op jit(solution)/shard_map/all_to_all | solution.py:39
  125.6 2.3 %bitcast_reduce_fusion = (f32[2,8,48]{2,0,1:T(2,128)S(1)}, f32[8,2,48,768]{3,2,1,0:T(8,128)S(1)}) fusion(bf16[2,8,48,128]{3,2,0,1:T(8,128)(2,1)S(1)} %reshape.320, bf16[8,768,256]{2,1,0:T(8,128)(2,1)} %bitcast.117), kind=kOutput, calls=%fused_computation.12 | convolution fusion | flops 152173824 | bytes 4131840 | tf_op jit(solution)/shard_map/tchd,cpd->tchp/dot_general | solution.py:159
  130.5 7.8 %all-to-all-done.4 = bf16[8,8,24,256]{3,2,1,0:T(8,128)(2,1)S(1)} async-done(((bf16[8,8,24,256]{3,2,1,0:T(8,128)(2,1)}), bf16[8,8,24,256]{3,2,1,0:T(8,128)(2,1)S(1)}, u32[]{:S(2)}, u32[]{:S(2)}) %all-to-all-start.4) | async-done | bytes 786464 | tf_op jit(solution)/shard_map/all_to_all | solution.py:39
  138.4 0.9 multiply_reduce_fusion
  139.3 0.9 fusion
  140.2 0.9 fusion.23
  141.3 0.9 reshape.317
  (81 shorter events, 14.1 us)
Async XLA Ops:
  0.6 20.0 %copy-start = (bf16[768,256]{1,0:T(8,128)(2,1)S(1)}, bf16[768,256]{1,0:T(8,128)(2,1)}, u32[]{:S(2)}) copy-start(bf16[768,256]{1,0:T(8,128)(2,1)} %param.15) | copy-start | bytes 1179652
  0.6 34.6 %copy-start.3 = (bf16[125,256]{1,0:T(8,128)(2,1)S(1)}, bf16[125,256]{1,0:T(8,128)(2,1)}, u32[]{:S(2)}) copy-start(bf16[125,256]{1,0:T(8,128)(2,1)} %param.20) | copy-start | bytes 192004
  0.7 35.8 %copy-start.1 = (bf16[125,768]{1,0:T(8,128)(2,1)S(1)}, bf16[125,768]{1,0:T(8,128)(2,1)}, u32[]{:S(2)}) copy-start(bf16[125,768]{1,0:T(8,128)(2,1)} %param.19) | copy-start | bytes 576004
  2.9 25.6 %all-to-all-start = ((s32[64,1,4]{2,1,0:T(1,128)}), s32[64,1,4]{2,1,0:T(1,128)S(1)}, u32[]{:S(2)}, u32[]{:S(2)}) async-start(s32[64,1,4]{2,1,0:T(1,128)} %bitcast), calls=%async_computation | async-start | bytes 65536 | tf_op jit(solution)/shard_map/all_to_all | solution.py:114
  28.5 12.8 %all-to-all-start.2 = ((f32[8,24,257]{2,1,0:T(8,128)}), f32[8,24,257]{2,1,0:T(8,128)S(1)}, u32[]{:S(2)}, u32[]{:S(2)}) async-start(f32[8,24,257]{2,1,0:T(8,128)} %pad_maximum_fusion.1), calls=%async_computation.2 | async-start | bytes 589824 | tf_op jit(solution)/shard_map/all_to_all | solution.py:22
  35.3 2.4 %copy-start.2 = (bf16[125,768]{1,0:T(8,128)(2,1)S(1)}, bf16[125,768]{1,0:T(8,128)(2,1)}, u32[]{:S(2)}) copy-start(bf16[125,768]{1,0:T(8,128)(2,1)} %param.18) | copy-start | bytes 576004
  40.8 44.0 %copy-start.5 = (s32[1,2,64]{2,1,0:T(2,128)S(1)}, s32[1,2,64]{2,1,0:T(2,128)}, u32[]{:S(2)}) copy-start(s32[1,2,64]{2,1,0:T(2,128)} %param.17) | copy-start | bytes 1540
  41.4 33.0 %all-to-all-start.1 = ((bf16[64,4,1792]{2,1,0:T(4,128)(2,1)}), bf16[64,4,1792]{2,1,0:T(4,128)(2,1)S(1)}, u32[]{:S(2)}, u32[]{:S(2)}) async-start(bf16[64,4,1792]{2,1,0:T(4,128)(2,1)} %pad_maximum_fusion), calls=%async_computation.1 | async-start | bytes 1835008 | tf_op jit(solution)/shard_map/all_to_all | solution.py:58
  75.3 32.7 %all-to-all-start.3 = ((bf16[64,24,256]{2,1,0:T(8,128)(2,1)}), bf16[64,24,256]{2,1,0:T(8,128)(2,1)S(1)}, u32[]{:S(2)}, u32[]{:S(2)}) async-start(bf16[64,24,256]{2,1,0:T(8,128)(2,1)} %broadcast_in_dim.142), calls=%async_computation.3 | async-start | bytes 1572864 | tf_op jit(solution)/shard_map/all_to_all | solution.py:39
  108.0 12.4 %all-to-all-start.5 = ((bf16[2,64,768]{2,0,1:T(2,128)(2,1)}), bf16[2,64,768]{2,0,1:T(2,128)(2,1)S(1)}, u32[]{:S(2)}, u32[]{:S(2)}) async-start(bf16[2,64,768]{2,0,1:T(2,128)(2,1)} %copy.54), calls=%async_computation.5 | async-start | bytes 393216 | tf_op jit(solution)/shard_map/all_to_all | solution.py:146
  121.3 17.0 %all-to-all-start.4 = ((bf16[8,8,24,256]{3,2,1,0:T(8,128)(2,1)}), bf16[8,8,24,256]{3,2,1,0:T(8,128)(2,1)S(1)}, u32[]{:S(2)}, u32[]{:S(2)}) async-start(bf16[8,8,24,256]{3,2,1,0:T(8,128)(2,1)} %broadcast_in_dim.144), calls=%async_computation.4 | async-start | bytes 1572864 | tf_op jit(solution)/shard_map/all_to_all | solution.py:39
  125.6 3.0 %copy-start.4 = (bf16[1,8,768,256]{3,2,1,0:T(8,128)(2,1)S(1)}, bf16[1,8,768,256]{3,2,1,0:T(8,128)(2,1)}, u32[]{:S(2)}) copy-start(bf16[1,8,768,256]{3,2,1,0:T(8,128)(2,1)} %param.21) | copy-start | bytes 9437188
where the time goes:
time: 143 us; the launch traced here: 142 us
  waiting for transfers between devices  65.2 us (46%)
  starting transfers between devices  46.7 us (33%)
  local copies, waits for them, and re-layouts  14.8 us (10%)
  other arithmetic  7.09 us (5%)
  matrix products  6.65 us (5%)
  between operations  1.74 us (1%)
    all_to_all x2, waiting for transfers between devices, copy_for_each(): lax.all_to_all(jnp.broadcast_to(shard[None], (length, *shard.shape)), axi...  26.4 us
    all_to_all x1, waiting for transfers between devices, in_one_piece(): lax.all_to_all(both, axis, split_axis=split_dim, concat_axis=concat_dim,...  24.8 us
    all_to_all x1, starting transfers between devices, body(): lax.all_to_all(request.reshape(wide_count, capacity), 'wide', split_axis=...  16.3 us
    all_to_all x2, starting transfers between devices, copy_for_each(): lax.all_to_all(jnp.broadcast_to(shard[None], (length, *shard.shape)), axi...  13.2 us
    all_to_all x1, waiting for transfers between devices, body(): lax.all_to_all(self_q.reshape(steps, cand, self_q.shape[1]), 'narrow', sp...  7.37 us
    all_to_all x1, starting transfers between devices, in_one_piece(): lax.all_to_all(both, axis, split_axis=split_dim, concat_axis=concat_dim,...  7.18 us
    all_to_all x1, waiting for transfers between devices, body(): lax.all_to_all(request.reshape(wide_count, capacity), 'wide', split_axis=...  5.97 us
    all_to_all x1, starting transfers between devices, sent_and_summed(): lax.all_to_all(pieces, axis, split_axis=0, concat_axis=0, tiled=True)  5.21 us
  transfers between devices with their start and end apart: 6, of which 6 were waited for; matrix products, arithmetic and copies ran while one was open for 14% of the time, Pallas kernels for 0%

commit v1 on v0

--- a/solution.py
+++ b/solution.py
@@ -143,12 +143,18 @@
     )
     cross_out = result.astype(jnp.bfloat16).reshape(1, steps, cand, heads_dev * HEAD)
     own_cand = cand // narrow_count
-    queries = lax.all_to_all(
-        self_q.reshape(steps, cand, self_q.shape[1]),
-        "narrow",
-        split_axis=1,
-        concat_axis=2,
-        tiled=True,
+    queries = jnp.concatenate(
+        lax.all_to_all(
+            jnp.stack(
+                jnp.split(
+                    self_q.reshape(steps, cand, self_q.shape[1]), lax.axis_size("narrow"), axis=1
+                )
+            ),
+            "narrow",
+            0,
+            0,
+        ),
+        axis=2,
     )
     queries = queries.reshape(steps, own_cand, HEADS, HEAD)
     fresh = lax.dynamic_slice_in_dim(

time: 143 us -> 143 us (level)
  local copies, waits for them, and re-layouts: 14.8 us -> 18.8 us
  waiting for transfers between devices: 65.2 us -> 61.3 us
    unnamed x13 -> x20, local copies, waits for them, and re-layouts: 0.77 us -> 5.05 us
    all_to_all x2, waiting for transfers between devices: 26.4 us -> 22.8 us  [copy_for_each(): lax.all_to_all(jnp.broadcast_to(shard[None], (length, *shard.shape)), axi...]
  transfers between devices with their start and end apart: 6 -> 6, of which waited for: 6 -> 6; matrix products, arithmetic and copies ran while one was open for 14% -> 17% of each run, Pallas kernels for 0% -> 0%
where the time goes in v1:
time: 143 us; the launch traced here: 142 us
  waiting for transfers between devices  61.3 us (43%)
  starting transfers between devices  46.5 us (33%)
  local copies, waits for them, and re-layouts  18.8 us (13%)
  other arithmetic  7.08 us (5%)
  matrix products  6.64 us (5%)
  between operations  1.73 us (1%)
    all_to_all x1, waiting for transfers between devices, in_one_piece(): lax.all_to_all(both, axis, split_axis=split_dim, concat_axis=concat_dim,...  24.6 us
    all_to_all x2, waiting for transfers between devices, copy_for_each(): lax.all_to_all(jnp.broadcast_to(shard[None], (length, *shard.shape)), axi...  22.8 us
    all_to_all x1, starting transfers between devices, body(): lax.all_to_all(request.reshape(wide_count, capacity), 'wide', split_axis=...  16.3 us
    all_to_all x2, starting transfers between devices, copy_for_each(): lax.all_to_all(jnp.broadcast_to(shard[None], (length, *shard.shape)), axi...  13.1 us
    all_to_all x1, waiting for transfers between devices, body(): lax.all_to_all(jnp.stack(jnp.split(self_q.reshape(steps, cand, self_q.sha...  7.37 us
    all_to_all x1, starting transfers between devices, in_one_piece(): lax.all_to_all(both, axis, split_axis=split_dim, concat_axis=concat_dim,...  7.18 us
    all_to_all x1, waiting for transfers between devices, body(): lax.all_to_all(request.reshape(wide_count, capacity), 'wide', split_axis=...  5.96 us
    all_to_all x1, starting transfers between devices, sent_and_summed(): lax.all_to_all(pieces, axis, split_axis=0, concat_axis=0, tiled=True)  5.21 us
  transfers between devices with their start and end apart: 6, of which 6 were waited for; matrix products, arithmetic and copies ran while one was open for 17% of the time, Pallas kernels for 0%

profile of v1, /device:TPU:24, one launch (start us, length us, event | category | flops | bytes accessed | tf_op | source)
XLA Modules:
  0.0 142.1 jit_solution(16929143206072249058)
XLA Ops:
  2.9 16.3 %all-to-all-start = ((s32[64,1,4]{2,1,0:T(1,128)}), s32[64,1,4]{2,1,0:T(1,128)S(1)}, u32[]{:S(2)}, u32[]{:S(2)}) async-start(s32[64,1,4]{2,1,0:T(1,128)} %bitcast), calls=%async_computation | async-start | bytes 65536 | tf_op jit(solution)/shard_map/all_to_all | solution.py:114
  19.3 1.1 fusion.27
  20.6 1.2 fusion.29
  22.6 6.0 %all-to-all-done = s32[64,1,4]{2,1,0:T(1,128)S(1)} async-done(((s32[64,1,4]{2,1,0:T(1,128)}), s32[64,1,4]{2,1,0:T(1,128)S(1)}, u32[]{:S(2)}, u32[]{:S(2)}) %all-to-all-start) | async-done | bytes 1056 | tf_op jit(solution)/shard_map/all_to_all | solution.py:114
  28.5 5.2 %all-to-all-start.2 = ((f32[8,24,257]{2,1,0:T(8,128)}), f32[8,24,257]{2,1,0:T(8,128)S(1)}, u32[]{:S(2)}, u32[]{:S(2)}) async-start(f32[8,24,257]{2,1,0:T(8,128)} %pad_maximum_fusion.1), calls=%async_computation.2 | async-start | bytes 589824 | tf_op jit(solution)/shard_map/all_to_all | solution.py:22
  35.3 1.2 gather_fusion
  36.5 1.2 gather_fusion.3
  37.7 1.2 gather_fusion.2
  39.5 1.3 pad_maximum_fusion
  41.4 7.2 %all-to-all-start.1 = ((bf16[64,4,1792]{2,1,0:T(4,128)(2,1)}), bf16[64,4,1792]{2,1,0:T(4,128)(2,1)S(1)}, u32[]{:S(2)}, u32[]{:S(2)}) async-start(bf16[64,4,1792]{2,1,0:T(4,128)(2,1)} %pad_maximum_fusion), calls=%async_computation.1 | async-start | bytes 1835008 | tf_op jit(solution)/shard_map/all_to_all | solution.py:58
  49.9 24.6 %all-to-all-done.1 = bf16[64,4,1792]{2,1,0:T(4,128)(2,1)S(1)} async-done(((bf16[64,4,1792]{2,1,0:T(4,128)(2,1)}), bf16[64,4,1792]{2,1,0:T(4,128)(2,1)S(1)}, u32[]{:S(2)}, u32[]{:S(2)}) %all-to-all-start.1) | async-done | bytes 917536 | tf_op jit(solution)/shard_map/all_to_all | solution.py:58
  74.5 0.9 broadcast_in_dim.142
  75.4 9.3 %all-to-all-start.3 = ((bf16[64,24,256]{2,1,0:T(8,128)(2,1)}), bf16[64,24,256]{2,1,0:T(8,128)(2,1)S(1)}, u32[]{:S(2)}, u32[]{:S(2)}) async-start(bf16[64,24,256]{2,1,0:T(8,128)(2,1)} %broadcast_in_dim.142), calls=%async_computation.3 | async-start | bytes 1572864 | tf_op jit(solution)/shard_map/all_to_all | solution.py:39
  92.9 15.0 %all-to-all-done.3 = bf16[64,24,256]{2,1,0:T(8,128)(2,1)S(1)} async-done(((bf16[64,24,256]{2,1,0:T(8,128)(2,1)}), bf16[64,24,256]{2,1,0:T(8,128)(2,1)S(1)}, u32[]{:S(2)}, u32[]{:S(2)}) %all-to-all-start.3) | async-done | bytes 786464 | tf_op jit(solution)/shard_map/all_to_all | solution.py:39
  107.9 4.7 %all-to-all-start.5 = ((bf16[8,2,8,768]{3,2,1,0:T(8,128)(2,1)}), bf16[8,2,8,768]{3,2,1,0:T(8,128)(2,1)S(1)}, u32[]{:S(2)}, u32[]{:S(2)}) async-start(bf16[8,2,8,768]{3,2,1,0:T(8,128)(2,1)} %fusion.34), calls=%async_computation.5 | async-start | bytes 393216 | tf_op jit(solution)/shard_map/all_to_all | solution.py:147
  112.9 7.4 %all-to-all-done.5 = bf16[8,2,8,768]{3,2,1,0:T(8,128)(2,1)S(1)} async-done(((bf16[8,2,8,768]{3,2,1,0:T(8,128)(2,1)}), bf16[8,2,8,768]{3,2,1,0:T(8,128)(2,1)S(1)}, u32[]{:S(2)}, u32[]{:S(2)}) %all-to-all-start.5) | async-done | bytes 196640 | tf_op jit(solution)/shard_map/all_to_all | solution.py:147
  120.3 0.9 broadcast_in_dim.144
  121.2 3.7 %all-to-all-start.4 = ((bf16[8,8,24,256]{3,2,1,0:T(8,128)(2,1)}), bf16[8,8,24,256]{3,2,1,0:T(8,128)(2,1)S(1)}, u32[]{:S(2)}, u32[]{:S(2)}) async-start(bf16[8,8,24,256]{3,2,1,0:T(8,128)(2,1)} %broadcast_in_dim.144), calls=%async_computation.4 | async-start | bytes 1572864 | tf_op jit(solution)/shard_map/all_to_all | solution.py:39
  125.5 2.3 %bitcast_reduce_fusion = (f32[2,8,48]{2,0,1:T(2,128)S(1)}, f32[8,2,48,768]{3,2,1,0:T(8,128)S(1)}) fusion(bf16[2,8,48,128]{3,2,0,1:T(8,128)(2,1)S(1)} %reshape_reshape.7, bf16[8,768,256]{2,1,0:T(8,128)(2,1)} %bitcast.152), kind=kOutput, calls=%fused_computation.12 | convolution fusion | flops 152173824 | bytes 4131840 | tf_op jit(solution)/shard_map/tchd,cpd->tchp/dot_general | solution.py:165
  130.4 7.9 %all-to-all-done.4 = bf16[8,8,24,256]{3,2,1,0:T(8,128)(2,1)S(1)} async-done(((bf16[8,8,24,256]{3,2,1,0:T(8,128)(2,1)}), bf16[8,8,24,256]{3,2,1,0:T(8,128)(2,1)S(1)}, u32[]{:S(2)}, u32[]{:S(2)}) %all-to-all-start.4) | async-done | bytes 786464 | tf_op jit(solution)/shard_map/all_to_all | solution.py:39
  138.3 0.9 multiply_reduce_fusion
  139.2 0.9 fusion
  140.1 0.9 fusion.23
  141.2 0.9 reshape.316
  (86 shorter events, 18.1 us)
Async XLA Ops:
  0.6 20.0 %copy-start = (bf16[768,256]{1,0:T(8,128)(2,1)S(1)}, bf16[768,256]{1,0:T(8,128)(2,1)}, u32[]{:S(2)}) copy-start(bf16[768,256]{1,0:T(8,128)(2,1)} %param.15) | copy-start | bytes 1179652
  0.6 34.6 %copy-start.3 = (bf16[125,256]{1,0:T(8,128)(2,1)S(1)}, bf16[125,256]{1,0:T(8,128)(2,1)}, u32[]{:S(2)}) copy-start(bf16[125,256]{1,0:T(8,128)(2,1)} %param.20) | copy-start | bytes 192004
  0.7 35.8 %copy-start.1 = (bf16[125,768]{1,0:T(8,128)(2,1)S(1)}, bf16[125,768]{1,0:T(8,128)(2,1)}, u32[]{:S(2)}) copy-start(bf16[125,768]{1,0:T(8,128)(2,1)} %param.19) | copy-start | bytes 576004
  2.9 25.6 %all-to-all-start = ((s32[64,1,4]{2,1,0:T(1,128)}), s32[64,1,4]{2,1,0:T(1,128)S(1)}, u32[]{:S(2)}, u32[]{:S(2)}) async-start(s32[64,1,4]{2,1,0:T(1,128)} %bitcast), calls=%async_computation | async-start | bytes 65536 | tf_op jit(solution)/shard_map/all_to_all | solution.py:114
  28.5 12.8 %all-to-all-start.2 = ((f32[8,24,257]{2,1,0:T(8,128)}), f32[8,24,257]{2,1,0:T(8,128)S(1)}, u32[]{:S(2)}, u32[]{:S(2)}) async-start(f32[8,24,257]{2,1,0:T(8,128)} %pad_maximum_fusion.1), calls=%async_computation.2 | async-start | bytes 589824 | tf_op jit(solution)/shard_map/all_to_all | solution.py:22
  35.3 2.4 %copy-start.2 = (bf16[125,768]{1,0:T(8,128)(2,1)S(1)}, bf16[125,768]{1,0:T(8,128)(2,1)}, u32[]{:S(2)}) copy-start(bf16[125,768]{1,0:T(8,128)(2,1)} %param.18) | copy-start | bytes 576004
  39.4 9.9 %copy-start.5 = (s32[1,2,64]{2,1,0:T(2,128)S(1)}, s32[1,2,64]{2,1,0:T(2,128)}, u32[]{:S(2)}) copy-start(s32[1,2,64]{2,1,0:T(2,128)} %param.17) | copy-start | bytes 1540
  41.4 33.1 %all-to-all-start.1 = ((bf16[64,4,1792]{2,1,0:T(4,128)(2,1)}), bf16[64,4,1792]{2,1,0:T(4,128)(2,1)S(1)}, u32[]{:S(2)}, u32[]{:S(2)}) async-start(bf16[64,4,1792]{2,1,0:T(4,128)(2,1)} %pad_maximum_fusion), calls=%async_computation.1 | async-start | bytes 1835008 | tf_op jit(solution)/shard_map/all_to_all | solution.py:58
  75.4 32.5 %all-to-all-start.3 = ((bf16[64,24,256]{2,1,0:T(8,128)(2,1)}), bf16[64,24,256]{2,1,0:T(8,128)(2,1)S(1)}, u32[]{:S(2)}, u32[]{:S(2)}) async-start(bf16[64,24,256]{2,1,0:T(8,128)(2,1)} %broadcast_in_dim.142), calls=%async_computation.3 | async-start | bytes 1572864 | tf_op jit(solution)/shard_map/all_to_all | solution.py:39
  107.9 12.4 %all-to-all-start.5 = ((bf16[8,2,8,768]{3,2,1,0:T(8,128)(2,1)}), bf16[8,2,8,768]{3,2,1,0:T(8,128)(2,1)S(1)}, u32[]{:S(2)}, u32[]{:S(2)}) async-start(bf16[8,2,8,768]{3,2,1,0:T(8,128)(2,1)} %fusion.34), calls=%async_computation.5 | async-start | bytes 393216 | tf_op jit(solution)/shard_map/all_to_all | solution.py:147
  121.2 17.0 %all-to-all-start.4 = ((bf16[8,8,24,256]{3,2,1,0:T(8,128)(2,1)}), bf16[8,8,24,256]{3,2,1,0:T(8,128)(2,1)S(1)}, u32[]{:S(2)}, u32[]{:S(2)}) async-start(bf16[8,8,24,256]{3,2,1,0:T(8,128)(2,1)} %broadcast_in_dim.144), calls=%async_computation.4 | async-start | bytes 1572864 | tf_op jit(solution)/shard_map/all_to_all | solution.py:39
  125.5 3.0 %copy-start.4 = (bf16[1,8,768,256]{3,2,1,0:T(8,128)(2,1)S(1)}, bf16[1,8,768,256]{3,2,1,0:T(8,128)(2,1)}, u32[]{:S(2)}) copy-start(bf16[1,8,768,256]{3,2,1,0:T(8,128)(2,1)} %param.21) | copy-start | bytes 9437188
